TPU v7x, 32 devices: a whole 2x2x4 slice. The times are simulated.
32 devices in a mesh: dp: 8 (over z, core), mp: 4 (over y, x).
Axes of the slice: x: 2, y: 2, z: 4, core: 2. Of those that a mesh axis runs over, the one named last changes fastest.
Arguments:
- master: float32 [4096, 5120], P('dp', 'mp'), may hold values from -60 to 60
- moment_first: float32 [4096, 5120], P('dp', 'mp'), may hold values from -0.06 to 0.06
- moment_second: float32 [4096, 5120], P('dp', 'mp'), may hold values from 1e-05 to 0.001
- gradients: float32 [4096, 5120], P('dp', 'mp'), may hold values from -0.2 to 0.2
- step_count: int32 [1], replicated, may hold values from 1 to 10
- tensor_rows: int32 [24], replicated, may hold values from 1 to 1024, 4096 in all
- decay_mask: int32 [24], replicated, may hold values 0 or 1
Outputs:
- new_master: float32 [4096, 5120], P('dp', 'mp')
- new_first: float32 [4096, 5120], P('dp', 'mp')
- new_second: float32 [4096, 5120], P('dp', 'mp')
- compute_weights: bfloat16 [4096, 5120], P(None, 'mp')
Inputs may be any that keep to these rules, and one draw needn't show every extreme that they name: `tensor_rows`: the rows sum to 4096; the largest tensor has 1024 rows.
All inputs are finite; a program needn't handle non-finite values.
Results may differ from a plain program's by a relative error of at most 0.0004.
Values may be sent and summed in bfloat16 or wider, within the bound.
A program may use at most 128 MiB of HBM per device.

v0:
```python
import jax
import jax.numpy as jnp
from jax import lax
from jax.sharding import PartitionSpec as P

beta_first = 0.9
beta_second = 0.999
adam_epsilon = 1e-06
decay_rate = 0.3
learn_rate = 0.3
norm_epsilon = 1e-06


def membership(first_row, count, offsets, tensor_rows):
    row_ids = first_row + jnp.arange(count, dtype=jnp.int32)
    inside = (row_ids[None, :] >= offsets[:, None]) & (
        row_ids[None, :] < (offsets + tensor_rows)[:, None]
    )
    return inside.astype(jnp.float32)


def local(master, moment_first, moment_second, gradients, step_count, tensor_rows, decay_mask):
    rows_dev = master.shape[0]
    steps = step_count[0].astype(jnp.float32)
    new_first = beta_first * moment_first + (1.0 - beta_first) * gradients
    new_second = beta_second * moment_second + (1.0 - beta_second) * gradients * gradients
    fix_first = 1.0 - jnp.power(jnp.float32(beta_first), steps)
    fix_second = 1.0 - jnp.power(jnp.float32(beta_second), steps)
    offsets = jnp.cumsum(tensor_rows) - tensor_rows
    first_row = lax.axis_index("dp") * rows_dev
    member = membership(first_row, rows_dev, offsets, tensor_rows)
    mask_rows = jnp.dot(decay_mask.astype(jnp.float32), member, precision=lax.Precision.HIGHEST)
    update = new_first / fix_first / (jnp.sqrt(new_second / fix_second) + adam_epsilon)
    update = update + decay_rate * mask_rows[:, None] * master
    weight_part = jnp.dot(member, jnp.sum(master * master, axis=1), precision=lax.Precision.HIGHEST)
    update_part = jnp.dot(member, jnp.sum(update * update, axis=1), precision=lax.Precision.HIGHEST)
    column_sums = lax.psum((weight_part, update_part), "mp")
    weight_sq, update_sq = lax.psum((column_sums[0], column_sums[1]), "dp")
    ratio = jnp.sqrt(weight_sq) / (jnp.sqrt(update_sq) + norm_epsilon)
    ratio_rows = jnp.dot(ratio, member, precision=lax.Precision.HIGHEST)
    new_master = master - learn_rate * ratio_rows[:, None] * update
    compute_weights = lax.all_gather(new_master.astype(jnp.bfloat16), "dp", axis=0, tiled=True)
    return (new_master, new_first, new_second, compute_weights)


def solution(mesh):
    placed = (P("dp", "mp"), P("dp", "mp"), P("dp", "mp"), P("dp", "mp"), P(), P(), P())
    return jax.shard_map(
        local,
        mesh=mesh,
        in_specs=placed,
        out_specs=(P("dp", "mp"), P("dp", "mp"), P("dp", "mp"), P(None, "mp")),
        check_vma=False,
    )
```

profile of v0, /device:TPU:0, one launch (start us, length us, event | category | flops | bytes accessed | tf_op | source)
XLA Modules:
  0.0 159.5 jit_solution(13009378844300602519)
XLA Ops:
  7.2 0.0 all-gather.2.cloned.1.call-start
  8.0 0.7 copy.12
  8.7 0.1 reduce
  8.9 0.7 sub.18
  9.5 0.1 compare_and_fusion
  9.6 0.8 fusion.2
  10.4 0.0 copy-start
  10.4 7.1 %multiply_reduce_fusion = (f32[512]{0:T(512)S(1)}, f32[512,1280]{1,0:T(8,128)}, f32[512,1280]{1,0:T(8,128)}, f32[512,1280]{1,0:T(8,128)}, f32[512]{0:T(512)S(1)}) fusion(f32[512,1280]{1,0:T(8,128)} %param.7, f32[512]{0:T(512)S(1)} %broadcast_multiply_fusion.1, f32[]{:T(128)} %bitcast.4, f32[]{:T(128)} %bitcast.3, f32[512,1280]{1,0:T(8,128)} %param.10, ...), kind=kLoop, calls=%fused_computation.3 | loop fusion | flops 11140096 | bytes 18356232 | tf_op jit(solution)/shard_map/reduce_sum | solution.py:36
  17.5 0.1 convolution_bitcast_fusion
  17.6 0.1 convolution_bitcast_fusion.1
  17.7 11.4 %all-reduce.1 = (f32[24]{0:T(128)S(1)}, f32[24]{0:T(128)S(1)}) all-reduce(f32[24]{0:T(128)S(1)} %convolution_bitcast_fusion, f32[24]{0:T(128)S(1)} %convolution_bitcast_fusion.1), channel_id=1, replica_groups=mesh['dp'=8,'mp'=4] {'mp'}, use_global_device_ids=true, to_apply=%region_5.6 | all-reduce | flops 48 | bytes 384 | tf_op jit(solution)/shard_map/psum | solution.py:37
  29.1 14.6 %all-reduce = (f32[24]{0:T(128)S(1)}, f32[24]{0:T(128)S(1)}) all-reduce(f32[24]{0:T(128)S(1)} %get-tuple-element.6, f32[24]{0:T(128)S(1)} %get-tuple-element.7), channel_id=1, replica_groups=mesh['dp'=8,'mp'=4] {'dp'}, use_global_device_ids=true, to_apply=%region_6.7 | all-reduce | flops 48 | bytes 384 | tf_op jit(solution)/shard_map/psum | solution.py:38
  43.7 0.1 fusion.3
  43.9 0.0 copy-done
  43.9 4.0 %fusion.7 = (bf16[512,1280]{1,0:T(8,128)(2,1)}, f32[512,1280]{1,0:T(8,128)}) fusion(f32[512,1280]{1,0:T(8,128)S(1)} %copy-done, f32[512,1280]{1,0:T(8,128)} %get-tuple-element.11, f32[512]{0:T(512)S(1)} %broadcast_multiply_fusion), kind=kLoop, calls=%fused_computation.20 | loop fusion | flops 1966080 | bytes 9177088 | tf_op jit(solution)/shard_map/convert_element_type | solution.py:42
  47.9 0.0 all-gather.2.cloned.1.call-update
  47.9 96.0 %all-gather.2.cloned.1.call-done = bf16[4096,1280]{1,0:T(8,128)(2,1)} async-done(((bf16[512,1280]{1,0:T(8,128)(2,1)}), bf16[4096,1280]{1,0:T(8,128)(2,1)}) %all-gather.2.cloned.1.call-update) | async-done | bytes 10485776 | tf_op jit(solution)/shard_map/all_gather | solution.py:42
  144.0 8.7 %copy.15 = bf16[4096,1280]{1,0:T(8,128)(2,1)} copy(bf16[4096,1280]{1,0:T(8,128)(2,1)} %all-gather.2.cloned.1.call-done) | data formatting | bytes 20971520
  (4 shorter events, 0.1 us)
Async XLA Ops:
  7.2 136.8 %all-gather.2.cloned.1.call-start = ((), (), s32[]{:S(2)}) async-start(), calls=%async_computation | async-start | bytes 11796480 | tf_op jit(solution)/shard_map/all_gather | solution.py:42
  10.4 33.5 %copy-start = (f32[512,1280]{1,0:T(8,128)S(1)}, f32[512,1280]{1,0:T(8,128)}, u32[]{:S(2)}) copy-start(f32[512,1280]{1,0:T(8,128)} %param.7) | copy-start | bytes 7864324
Sparse Core Ops, SparseCore 0:
  48.1 95.8 all-gather.1
where the time goes:
time: 160 us
  waiting for transfers between devices  96 us (60%)
  blocking collectives  26 us (16%)
  between operations  14.8 us (9%)
  other arithmetic  12 us (8%)
  local copies, waits for them, and re-layouts  9.48 us (6%)
    all_gather x1, waiting for transfers between devices, local(): lax.all_gather(new_master.astype(jnp.bfloat16), 'dp', axis=0, tiled=True)  96 us
    psum x1, blocking collectives, local(): weight_sq, update_sq = lax.psum((column_sums[0], column_sums[1]), 'dp')  14.6 us
    psum x1, blocking collectives, local(): column_sums = lax.psum((weight_part, update_part), 'mp')  11.4 us
    unnamed x3, local copies, waits for them, and re-layouts  8.74 us
    reduce_sum x1, other arithmetic, local(): jnp.sum(update * update, axis=1)  7.08 us
    convert_element_type x1, other arithmetic, local(): new_master.astype(jnp.bfloat16)  4.02 us
  transfers between devices with their start and end apart: 1, of which 1 were waited for; matrix products, arithmetic and copies ran while one was open for 0% of the time, Pallas kernels for 0%

commit v1 on v0

v1 whole, which is shorter than its diff:
```python
import functools

import jax
import jax.numpy as jnp
from jax import lax
from jax.experimental import pallas as pl
from jax.experimental.pallas import tpu as pltpu
from jax.sharding import PartitionSpec as P

MESH = pl.DeviceIdType.MESH

beta_first = 0.9
beta_second = 0.999
adam_epsilon = 1e-06
decay_rate = 0.3
learn_rate = 0.3
norm_epsilon = 1e-06

LOADS = 8
CHUNKS = 4
GROUP = 16
HALF = 64


def power(base, exponent):
    result = jnp.float32(1.0)
    factor = jnp.float32(base)
    for bit in range(31):
        taken = ((exponent >> bit) & 1) == 1
        result = jnp.where(taken, result * factor, result)
        factor = factor * factor
    return result


def kernel(dp, mp, tensors, step_ref, rows_ref, mask_ref, m_hbm, f_hbm, s_hbm, g_hbm,
           nm_ref, nf_ref, ns_ref, x_ref,
           mb, fb, sb, gb, mine, mp_buf, mine2, dp_buf,
           load_sem, mp_send, mp_recv, dp_send, dp_recv,
           up_send, up_recv, down_send, down_recv, sib_send, sib_recv):
    rows, wide = m_hbm.shape
    me = lax.axis_index("dp")
    col = lax.axis_index("mp")
    chips = dp // 2
    chip, core = me // 2, me % 2
    sibling = me + 1 - 2 * core
    piece = rows // LOADS
    part = rows // CHUNKS

    def loads(i):
        at = pl.ds(i * piece, piece)
        pairs = ((m_hbm, mb), (f_hbm, fb), (s_hbm, sb), (g_hbm, gb))
        return [pltpu.make_async_copy(a.at[at], b.at[at], load_sem.at[n, i]) for n, (a, b) in enumerate(pairs)]

    for i in range(LOADS):
        for copy in loads(i):
            copy.start()

    barrier = pltpu.get_barrier_semaphore()
    for d in range(1, mp):
        pl.semaphore_signal(barrier, inc=1, device_id={"mp": lax.rem(col + d, mp)}, device_id_type=MESH)
    for d in range(1, dp):
        pl.semaphore_signal(barrier, inc=1, device_id={"dp": lax.rem(me + d, dp)}, device_id_type=MESH)

    step = step_ref[0]
    fix_first = 1.0 - power(beta_first, step)
    fix_second = 1.0 - power(beta_second, step)
    tile = (8, 128)
    scale = (jnp.full(tile, fix_first, jnp.float32) * lax.rsqrt(jnp.full(tile, fix_second, jnp.float32)))[0, 0]
    shift = fix_first * adam_epsilon

    lane = lax.broadcasted_iota(jnp.int32, (1, 128), 1)
    low = jnp.full((1, 128), -1, jnp.int32)
    high = jnp.full((1, 128), -1, jnp.int32)
    decay = jnp.zeros((1, 128), jnp.float32)
    offset = jnp.int32(0)
    for k in range(tensors):
        here = (lane == k) | (lane == HALF + k)
        after = offset + rows_ref[k]
        low = jnp.where(here, offset, low)
        high = jnp.where(here, after, high)
        decay = jnp.where(lane == k, decay_rate * mask_ref[k].astype(jnp.float32), decay)
        offset = after
    first_half = lane < HALF

    def member(start):
        ids = me * rows + start + lax.broadcasted_iota(jnp.int32, (GROUP, 128), 0)
        return ((ids >= low) & (ids < high)).astype(jnp.float32)

    def stats(i, total):
        at = pl.ds(pl.multiple_of(i * GROUP, GROUP), GROUP)
        inside = member(i * GROUP)
        decay_rows = jnp.sum(inside * decay, axis=1, keepdims=True)
        master, gradient = mb[at], gb[at]
        new_first = beta_first * fb[at] + (1.0 - beta_first) * gradient
        new_second = beta_second * sb[at] + (1.0 - beta_second) * gradient * gradient
        nf_ref[at] = new_first
        ns_ref[at] = new_second
        update = new_first / (scale * jnp.sqrt(new_second) + shift) + decay_rows * master
        gb[at] = update
        weight_sq = jnp.sum(master * master, axis=1, keepdims=True)
        update_sq = jnp.sum(update * update, axis=1, keepdims=True)
        return total + inside * jnp.where(first_half, weight_sq, update_sq)

    total = jnp.zeros((GROUP, 128), jnp.float32)
    steps = piece // GROUP
    for i in range(LOADS):
        for copy in loads(i):
            copy.wait()
        total = lax.fori_loop(i * steps, (i + 1) * steps, stats, total)
    total = jnp.sum(total, axis=0, keepdims=True)

    pl.semaphore_wait(barrier, mp + dp - 2)

    def exchange(axis, count, own, value, source, slots, send, recv):
        source[0] = value
        slots[own] = value
        copies = []
        for d in range(1, count):
            copies.append(pltpu.make_async_remote_copy(
                src_ref=source.at[0], dst_ref=slots.at[own], send_sem=send.at[d], recv_sem=recv.at[d],
                device_id={axis: lax.rem(own + d, count)}, device_id_type=MESH))
        for copy in copies:
            copy.start()
        for copy in copies:
            copy.wait_recv()
        result = slots[0]
        for j in range(1, count):
            result = result + slots[j]
        return result, copies

    total, mp_copies = exchange("mp", mp, col, total, mine, mp_buf, mp_send, mp_recv)
    total, dp_copies = exchange("dp", dp, me, total, mine2, dp_buf, dp_send, dp_recv)
    root = jnp.sqrt(jnp.broadcast_to(total, tile))
    ratio = root / (pltpu.roll(root, HALF, 1) + norm_epsilon)
    ratio = jnp.where(first_half, learn_rate * ratio[0:1], 0.0)

    def block(owner, k):
        return x_ref.at[pl.ds(pl.multiple_of(owner * rows + k * part, part), part)]

    def up(s, k):
        ref = block(me - 2 * s, k)
        return pltpu.make_async_remote_copy(
            src_ref=ref, dst_ref=ref, send_sem=up_send.at[s, k], recv_sem=up_recv.at[s, k],
            device_id={"dp": me + 2}, device_id_type=MESH)

    def down(s, k):
        ref = block(me + 2 * s, k)
        return pltpu.make_async_remote_copy(
            src_ref=ref, dst_ref=ref, send_sem=down_send.at[s, k], recv_sem=down_recv.at[s, k],
            device_id={"dp": me - 2}, device_id_type=MESH)

    def side(j, k):
        ref = block(2 * j + core, k)
        return pltpu.make_async_remote_copy(
            src_ref=ref, dst_ref=ref, send_sem=sib_send.at[j, k], recv_sem=sib_recv.at[j, k],
            device_id={"dp": sibling}, device_id_type=MESH)

    def arrival(recv, s, owner, k, to):
        ref = block(owner, k)
        return pltpu.make_async_remote_copy(
            src_ref=ref, dst_ref=ref, send_sem=up_send.at[0, k], recv_sem=recv.at[s, k],
            device_id={"dp": to}, device_id_type=MESH)

    last = chips - 1

    def final(i, carry):
        at = pl.ds(pl.multiple_of(i * GROUP, GROUP), GROUP)
        rate = jnp.sum(member(i * GROUP) * ratio, axis=1, keepdims=True)
        new_master = mb[at] - rate * gb[at]
        nm_ref[at] = new_master
        x_ref[pl.ds(pl.multiple_of(me * rows + i * GROUP, GROUP), GROUP)] = new_master.astype(jnp.bfloat16)
        return carry

    def send_own(k):
        @pl.when(chip < last)
        def _():
            up(0, k).start()

        @pl.when(chip > 0)
        def _():
            down(0, k).start()

        side(chip, k).start()

    groups = part // GROUP
    for k in range(CHUNKS):
        lax.fori_loop(k * groups, (k + 1) * groups, final, 0)
        if k > 0:
            send_own(k - 1)
    for copy in mp_copies + dp_copies:
        copy.wait_send()
    send_own(CHUNKS - 1)

    for s in range(last):
        for k in range(CHUNKS):
            @pl.when(s < chip)
            def _():
                arrival(up_recv, s, me - 2 * (s + 1), k, sibling).wait_recv()

                @pl.when(chip < last)
                def _():
                    up(s + 1, k).start()

                side(chip - (s + 1), k).start()

            @pl.when(s < last - chip)
            def _():
                arrival(down_recv, s, me + 2 * (s + 1), k, sibling).wait_recv()

                @pl.when(chip > 0)
                def _():
                    down(s + 1, k).start()

                side(chip + (s + 1), k).start()

    for s in range(chips):
        for k in range(CHUNKS):
            if s < last or last == 0:
                @pl.when((chip < last) & (s <= chip))
                def _():
                    up(s, k).wait_send()

                @pl.when((chip > 0) & (s <= last - chip))
                def _():
                    down(s, k).wait_send()

            side(s, k).wait_send()
            arrival(sib_recv, s, 2 * s + 1 - core, k, sibling).wait_recv()


def solution(mesh):
    dp, mp = mesh.shape["dp"], mesh.shape["mp"]

    def local(master, moment_first, moment_second, gradients, step_count, tensor_rows, decay_mask):
        rows, wide = master.shape
        tensors = tensor_rows.shape[0]
        chips = dp // 2
        full = pltpu.VMEM((rows, wide), jnp.float32)
        dma = pltpu.SemaphoreType.DMA
        hops = max(chips - 1, 1)
        return pl.pallas_call(
            functools.partial(kernel, dp, mp, tensors),
            out_shape=(full, full, full, pltpu.VMEM((dp * rows, wide), jnp.bfloat16)),
            in_specs=[pl.BlockSpec(memory_space=pltpu.SMEM)] * 3 + [pl.BlockSpec(memory_space=pltpu.HBM)] * 4,
            out_specs=(pl.BlockSpec(memory_space=pltpu.VMEM),) * 4,
            scratch_shapes=[
                full, full, full, full,
                pltpu.VMEM((1, 1, 128), jnp.float32),
                pltpu.VMEM((mp, 1, 128), jnp.float32),
                pltpu.VMEM((1, 1, 128), jnp.float32),
                pltpu.VMEM((dp, 1, 128), jnp.float32),
                dma((4, LOADS)), dma((mp,)), dma((mp,)), dma((dp,)), dma((dp,)),
                dma((hops, CHUNKS)), dma((hops, CHUNKS)), dma((hops, CHUNKS)), dma((hops, CHUNKS)),
                dma((chips, CHUNKS)), dma((chips, CHUNKS)),
            ],
            compiler_params=pltpu.CompilerParams(
                collective_id=0, has_side_effects=True, vmem_limit_bytes=20 * 1024 * 1024),
        )(step_count, tensor_rows, decay_mask, master, moment_first, moment_second, gradients)

    placed = (P("dp", "mp"), P("dp", "mp"), P("dp", "mp"), P("dp", "mp"), P(), P(), P())
    return jax.shard_map(
        local,
        mesh=mesh,
        in_specs=placed,
        out_specs=(P("dp", "mp"), P("dp", "mp"), P("dp", "mp"), P(None, "mp")),
        check_vma=False,
    )
```

time: 160 us -> 128 us (0.80)
  Pallas kernels: 0 us -> 110 us
  waiting for transfers between devices: 96 us -> 0 us
  blocking collectives: 26 us -> 0 us
  between operations: 14.8 us -> 1.3 us
  other arithmetic: 12 us -> 0 us
  local copies, waits for them, and re-layouts: 9.48 us -> 16.8 us
    pallas_call x0 -> x1, Pallas kernels: none -> 110 us  [local(): pl.pallas_call(functools.partial(kernel, dp, mp, tensors), out_shape=(ful...]
    all_gather x1 -> x0, waiting for transfers between devices: 96 us -> none  [local(): lax.all_gather(new_master.astype(jnp.bfloat16), 'dp', axis=0, tiled=True)]
    psum x2 -> x0, blocking collectives: 26 us -> none  [the longest x1 14.6 us: local(): weight_sq, update_sq = lax.psum((column_sums[0], column_sums[1]), 'dp')]
    unnamed x3 -> x16, local copies, waits for them, and re-layouts: 8.74 us -> 16.8 us
    reduce_sum x1 -> x0, other arithmetic: 7.08 us -> none  [local(): jnp.sum(update * update, axis=1)]
    convert_element_type x1 -> x0, other arithmetic: 4.02 us -> none  [local(): new_master.astype(jnp.bfloat16)]
  transfers between devices with their start and end apart: 1 -> 0, of which waited for: 1 -> 0; matrix products, arithmetic and copies ran while one was open for 0% -> 0% of each run, Pallas kernels for 0% -> 0%
where the time goes in v1:
time: 128 us
  Pallas kernels  110 us (86%)
  local copies, waits for them, and re-layouts  16.8 us (13%)
  between operations  1.3 us (1%)
    pallas_call x1, Pallas kernels, local(): pl.pallas_call(functools.partial(kernel, dp, mp, tensors), out_shape=(ful...  110 us
    unnamed x16, local copies, waits for them, and re-layouts  16.8 us

profile of v1, /device:TPU:0, one launch (start us, length us, event | category | flops | bytes accessed | tf_op | source)
XLA Modules:
  0.0 128.0 jit_solution(4095177351949268211)
XLA Ops:
  1.3 0.0 copy-start
  1.3 1.7 %copy-done = f32[512,1280]{1,0:T(8,128)S(1)} copy-done((f32[512,1280]{1,0:T(8,128)S(1)}, f32[512,1280]{1,0:T(8,128)}, u32[]{:S(2)}) %copy-start) | copy-done | bytes 2621464
  3.0 0.0 copy-start.1
  3.0 1.7 %copy-done.1 = f32[512,1280]{1,0:T(8,128)S(1)} copy-done((f32[512,1280]{1,0:T(8,128)S(1)}, f32[512,1280]{1,0:T(8,128)}, u32[]{:S(2)}) %copy-start.1) | copy-done | bytes 2621464
  4.8 0.0 copy-start.2
  4.8 1.7 %copy-done.2 = f32[512,1280]{1,0:T(8,128)S(1)} copy-done((f32[512,1280]{1,0:T(8,128)S(1)}, f32[512,1280]{1,0:T(8,128)}, u32[]{:S(2)}) %copy-start.2) | copy-done | bytes 2621464
  6.5 0.0 copy-start.3
  6.5 1.7 %copy-done.3 = f32[512,1280]{1,0:T(8,128)S(1)} copy-done((f32[512,1280]{1,0:T(8,128)S(1)}, f32[512,1280]{1,0:T(8,128)}, u32[]{:S(2)}) %copy-start.3) | copy-done | bytes 2621464
  8.2 0.0 copy-start.4
  8.2 0.7 copy-done.4
  8.9 0.0 copy-start.5
  8.9 0.7 copy-done.5
  9.6 109.9 %shard_map.102 = (f32[512,1280]{1,0:T(8,128)S(1)}, f32[512,1280]{1,0:T(8,128)S(1)}, f32[512,1280]{1,0:T(8,128)S(1)}, bf16[4096,1280]{1,0:T(8,128)(2,1)S(1)}) custom-call(s32[1]{0:T(128)S(6)} %copy.19.step_ref, s32[24]{0:T(128)S(1)} %copy-done.4, s32[24]{0:T(128)S(1)} %copy-done.5, f32[512,1280]{1,0:T(8,128)S(1)} %copy-done, f32[512,1280]{1,0:T(8,128)S(1)} %copy-done.1, ...), custom_call_target="tpu_custom_call" | custom-call | tf_op jit(solution)/shard_map/pallas_call | solution.py:241
  119.5 1.5 %copy.15 = f32[512,1280]{1,0:T(8,128)} copy(f32[512,1280]{1,0:T(8,128)S(1)} %get-tuple-element.4) | data formatting | bytes 5242880
  121.0 1.5 %copy.16 = f32[512,1280]{1,0:T(8,128)} copy(f32[512,1280]{1,0:T(8,128)S(1)} %get-tuple-element.5) | data formatting | bytes 5242880
  122.5 1.5 %copy.17 = f32[512,1280]{1,0:T(8,128)} copy(f32[512,1280]{1,0:T(8,128)S(1)} %get-tuple-element.6) | data formatting | bytes 5242880
  124.0 4.1 %copy.18 = bf16[4096,1280]{1,0:T(8,128)(2,1)} copy(bf16[4096,1280]{1,0:T(8,128)(2,1)S(1)} %get-tuple-element.7) | data formatting | bytes 20971520
Async XLA Ops:
  1.3 1.7 %copy-start = (f32[512,1280]{1,0:T(8,128)S(1)}, f32[512,1280]{1,0:T(8,128)}, u32[]{:S(2)}) copy-start(f32[512,1280]{1,0:T(8,128)} %m_hbm.1) | copy-start | bytes 7864324
  3.0 1.7 %copy-start.1 = (f32[512,1280]{1,0:T(8,128)S(1)}, f32[512,1280]{1,0:T(8,128)}, u32[]{:S(2)}) copy-start(f32[512,1280]{1,0:T(8,128)} %f_hbm.1) | copy-start | bytes 7864324
  4.8 1.7 %copy-start.2 = (f32[512,1280]{1,0:T(8,128)S(1)}, f32[512,1280]{1,0:T(8,128)}, u32[]{:S(2)}) copy-start(f32[512,1280]{1,0:T(8,128)} %s_hbm.1) | copy-start | bytes 7864324
  6.5 1.7 %copy-start.3 = (f32[512,1280]{1,0:T(8,128)S(1)}, f32[512,1280]{1,0:T(8,128)}, u32[]{:S(2)}) copy-start(f32[512,1280]{1,0:T(8,128)} %g_hbm.1) | copy-start | bytes 7864324
  8.2 0.7 copy-start.4
  8.9 0.7 copy-start.5

commit v2 on v1

--- a/solution.py
+++ b/solution.py
@@ -19,6 +19,7 @@
 LOADS = 8
 CHUNKS = 4
 GROUP = 16
+WRITES = 4
 HALF = 64
 
 
@@ -32,10 +33,10 @@
     return result
 
 
-def kernel(dp, mp, tensors, step_ref, rows_ref, mask_ref, m_hbm, f_hbm, s_hbm, g_hbm,
+def kernel(dp, mp, tensors, step_ref, rows_hbm, mask_hbm, m_hbm, f_hbm, s_hbm, g_hbm,
            nm_ref, nf_ref, ns_ref, x_ref,
-           mb, fb, sb, gb, mine, mp_buf, mine2, dp_buf,
-           load_sem, mp_send, mp_recv, dp_send, dp_recv,
+           mb, fb, sb, gb, mine, slots,
+           rows_ref, mask_ref, small_sem, load_sem, sum_send, sum_recv,
            up_send, up_recv, down_send, down_recv, sib_send, sib_recv):
     rows, wide = m_hbm.shape
     me = lax.axis_index("dp")
@@ -51,16 +52,31 @@
         pairs = ((m_hbm, mb), (f_hbm, fb), (s_hbm, sb), (g_hbm, gb))
         return [pltpu.make_async_copy(a.at[at], b.at[at], load_sem.at[n, i]) for n, (a, b) in enumerate(pairs)]
 
+    pairs = ((rows_hbm, rows_ref), (mask_hbm, mask_ref))
+    small = [pltpu.make_async_copy(a, b, small_sem.at[n]) for n, (a, b) in enumerate(pairs)]
+    for copy in small:
+        copy.start()
     for i in range(LOADS):
         for copy in loads(i):
             copy.start()
 
+    count = dp * mp
+    own = me * mp + col
+
+    def peer(d):
+        at = lax.rem(own + d, count)
+        return {"dp": at // mp, "mp": lax.rem(at, mp)}
+
     barrier = pltpu.get_barrier_semaphore()
-    for d in range(1, mp):
-        pl.semaphore_signal(barrier, inc=1, device_id={"mp": lax.rem(col + d, mp)}, device_id_type=MESH)
-    for d in range(1, dp):
-        pl.semaphore_signal(barrier, inc=1, device_id={"dp": lax.rem(me + d, dp)}, device_id_type=MESH)
-
+
+    def greet(d, carry):
+        pl.semaphore_signal(barrier, inc=1, device_id=peer(d), device_id_type=MESH)
+        return carry
+
+    lax.fori_loop(1, count, greet, 0)
+
+    for copy in small:
+        copy.wait()
     step = step_ref[0]
     fix_first = 1.0 - power(beta_first, step)
     fix_second = 1.0 - power(beta_second, step)
@@ -106,30 +122,33 @@
     for i in range(LOADS):
         for copy in loads(i):
             copy.wait()
-        total = lax.fori_loop(i * steps, (i + 1) * steps, stats, total)
+        total = lax.fori_loop(i * steps, (i + 1) * steps, stats, total, unroll=True)
     total = jnp.sum(total, axis=0, keepdims=True)
 
-    pl.semaphore_wait(barrier, mp + dp - 2)
-
-    def exchange(axis, count, own, value, source, slots, send, recv):
-        source[0] = value
-        slots[own] = value
-        copies = []
-        for d in range(1, count):
-            copies.append(pltpu.make_async_remote_copy(
-                src_ref=source.at[0], dst_ref=slots.at[own], send_sem=send.at[d], recv_sem=recv.at[d],
-                device_id={axis: lax.rem(own + d, count)}, device_id_type=MESH))
-        for copy in copies:
-            copy.start()
-        for copy in copies:
-            copy.wait_recv()
-        result = slots[0]
-        for j in range(1, count):
-            result = result + slots[j]
-        return result, copies
-
-    total, mp_copies = exchange("mp", mp, col, total, mine, mp_buf, mp_send, mp_recv)
-    total, dp_copies = exchange("dp", dp, me, total, mine2, dp_buf, dp_send, dp_recv)
+    pl.semaphore_wait(barrier, count - 1)
+
+    def share(d):
+        return pltpu.make_async_remote_copy(
+            src_ref=mine.at[0], dst_ref=slots.at[own], send_sem=sum_send.at[d], recv_sem=sum_recv.at[d],
+            device_id=peer(d), device_id_type=MESH)
+
+    def start_share(d, carry):
+        share(d).start()
+        return carry
+
+    def wait_share(d, carry):
+        share(d).wait_recv()
+        return carry
+
+    def sent_share(d, carry):
+        share(d).wait_send()
+        return carry
+
+    mine[0] = total
+    slots[own] = total
+    lax.fori_loop(1, count, start_share, 0)
+    lax.fori_loop(1, count, wait_share, 0)
+    total = jnp.sum(slots[...], axis=0)
     root = jnp.sqrt(jnp.broadcast_to(total, tile))
     ratio = root / (pltpu.roll(root, HALF, 1) + norm_epsilon)
     ratio = jnp.where(first_half, learn_rate * ratio[0:1], 0.0)
@@ -184,11 +203,10 @@
 
     groups = part // GROUP
     for k in range(CHUNKS):
-        lax.fori_loop(k * groups, (k + 1) * groups, final, 0)
+        lax.fori_loop(k * groups, (k + 1) * groups, final, 0, unroll=2)
         if k > 0:
             send_own(k - 1)
-    for copy in mp_copies + dp_copies:
-        copy.wait_send()
+    lax.fori_loop(1, count, sent_share, 0)
     send_own(CHUNKS - 1)
 
     for s in range(last):
@@ -226,6 +244,21 @@
 
             side(s, k).wait_send()
             arrival(sib_recv, s, 2 * s + 1 - core, k, sibling).wait_recv()
+
+
+def flush(*refs):
+    count = (len(refs) - 1) // 2
+    sems = refs[-1]
+    copies = []
+    for n, (source, target) in enumerate(zip(refs[:count], refs[count:2 * count])):
+        piece = source.shape[0] // WRITES
+        for i in range(WRITES):
+            at = pl.ds(i * piece, piece)
+            copies.append(pltpu.make_async_copy(source.at[at], target.at[at], sems.at[n, i]))
+    for copy in copies:
+        copy.start()
+    for copy in copies:
+        copy.wait()
 
 
 def solution(mesh):
@@ -238,24 +271,34 @@
         full = pltpu.VMEM((rows, wide), jnp.float32)
         dma = pltpu.SemaphoreType.DMA
         hops = max(chips - 1, 1)
-        return pl.pallas_call(
+        operands = (tensor_rows, decay_mask, master, moment_first, moment_second, gradients)
+        operands = [pltpu.with_memory_space_constraint(a, pltpu.HBM) for a in operands]
+        held = pl.pallas_call(
             functools.partial(kernel, dp, mp, tensors),
             out_shape=(full, full, full, pltpu.VMEM((dp * rows, wide), jnp.bfloat16)),
-            in_specs=[pl.BlockSpec(memory_space=pltpu.SMEM)] * 3 + [pl.BlockSpec(memory_space=pltpu.HBM)] * 4,
+            in_specs=[pl.BlockSpec(memory_space=pltpu.SMEM)] + [pl.BlockSpec(memory_space=pltpu.HBM)] * 6,
             out_specs=(pl.BlockSpec(memory_space=pltpu.VMEM),) * 4,
             scratch_shapes=[
                 full, full, full, full,
                 pltpu.VMEM((1, 1, 128), jnp.float32),
-                pltpu.VMEM((mp, 1, 128), jnp.float32),
-                pltpu.VMEM((1, 1, 128), jnp.float32),
-                pltpu.VMEM((dp, 1, 128), jnp.float32),
-                dma((4, LOADS)), dma((mp,)), dma((mp,)), dma((dp,)), dma((dp,)),
+                pltpu.VMEM((dp * mp, 1, 128), jnp.float32),
+                pltpu.SMEM(tensor_rows.shape, jnp.int32),
+                pltpu.SMEM(decay_mask.shape, jnp.int32), dma((2,)),
+                dma((4, LOADS)), dma((dp * mp,)), dma((dp * mp,)),
                 dma((hops, CHUNKS)), dma((hops, CHUNKS)), dma((hops, CHUNKS)), dma((hops, CHUNKS)),
                 dma((chips, CHUNKS)), dma((chips, CHUNKS)),
             ],
             compiler_params=pltpu.CompilerParams(
                 collective_id=0, has_side_effects=True, vmem_limit_bytes=20 * 1024 * 1024),
-        )(step_count, tensor_rows, decay_mask, master, moment_first, moment_second, gradients)
+        )(step_count, *operands)
+        return pl.pallas_call(
+            flush,
+            out_shape=tuple(jax.ShapeDtypeStruct(a.shape, a.dtype) for a in held),
+            in_specs=[pl.BlockSpec(memory_space=pltpu.VMEM)] * 4,
+            out_specs=(pl.BlockSpec(memory_space=pltpu.HBM),) * 4,
+            scratch_shapes=[dma((4, WRITES))],
+            compiler_params=pltpu.CompilerParams(vmem_limit_bytes=1024 * 1024),
+        )(*held)
 
     placed = (P("dp", "mp"), P("dp", "mp"), P("dp", "mp"), P("dp", "mp"), P(), P(), P())
     return jax.shard_map(

time: 128 us -> 110 us (0.86)
  local copies, waits for them, and re-layouts: 16.8 us -> 0 us
    unnamed x16 -> x0, local copies, waits for them, and re-layouts: 16.8 us -> none
    pallas_call x1, Pallas kernels: 110 us -> 103 us  [local(): pl.pallas_call(functools.partial(kernel, dp, mp, tensors), out_shape=(ful...]
    pallas_call x0 -> x1, Pallas kernels: none -> 6.49 us  [local(): pl.pallas_call(flush, out_shape=tuple((jax.ShapeDtypeStruct(a.shape, a.dt...]
where the time goes in v2:
time: 110 us
  Pallas kernels  109 us (99%)
  between operations  1.29 us (1%)
    pallas_call x1, Pallas kernels, local(): pl.pallas_call(functools.partial(kernel, dp, mp, tensors), out_shape=(ful...  103 us
    pallas_call x1, Pallas kernels, local(): pl.pallas_call(flush, out_shape=tuple((jax.ShapeDtypeStruct(a.shape, a.dt...  6.49 us

profile of v2, /device:TPU:0, one launch (start us, length us, event | category | flops | bytes accessed | tf_op | source)
XLA Modules:
  0.0 110.3 jit_solution(13696689904016776818)
XLA Ops:
  1.3 102.5 %shard_map.102 = (f32[512,1280]{1,0:T(8,128)S(1)}, f32[512,1280]{1,0:T(8,128)S(1)}, f32[512,1280]{1,0:T(8,128)S(1)}, bf16[4096,1280]{1,0:T(8,128)(2,1)S(1)}) custom-call(s32[1]{0:T(128)S(6)} %copy.11.step_ref, s32[24]{0:T(128)} %rows_hbm.1, s32[24]{0:T(128)} %mask_hbm.1, f32[512,1280]{1,0:T(8,128)} %m_hbm.1, f32[512,1280]{1,0:T(8,128)} %f_hbm.1, ...), custom_call_target="tpu_custom_call" | custom-call | tf_op jit(solution)/shard_map/pallas_call | solution.py:276
  103.8 6.5 %shard_map.103 = (f32[512,1280]{1,0:T(8,128)}, f32[512,1280]{1,0:T(8,128)}, f32[512,1280]{1,0:T(8,128)}, bf16[4096,1280]{1,0:T(8,128)(2,1)}) custom-call(f32[512,1280]{1,0:T(8,128)S(1)} %get-tuple-element.8.refs_0_, f32[512,1280]{1,0:T(8,128)S(1)} %get-tuple-element.9.refs_1_, f32[512,1280]{1,0:T(8,128)S(1)} %get-tuple-element.10.refs_2_, ...), custom_call_target="tpu_custom_call" | custom-call | tf_op jit(solution)/shard_map/pallas_call | solution.py:294
